TPU v7x, 32 devices: a whole 2x2x4 slice. The times are simulated.
32 devices in a mesh: gx: 16 (over z, y, x), gy: 1, gz: 2 (over core).
Axes of the slice: x: 2, y: 2, z: 4, core: 2. Of those that a mesh axis runs over, the one named last changes fastest.
Arguments:
- populations: float32 [19, 128, 8, 256], P(None, 'gx', 'gy', 'gz'), may hold values from 0.01 to 0.11
Outputs:
- populations_next: float32 [19, 128, 8, 256], P(None, 'gx', 'gy', 'gz')
- moments_slab: float32 [4, 256, 8, 128], P(None, ('gz', 'gx'), 'gy')
All inputs are finite; a program needn't handle non-finite values.
Results may differ from a plain program's by a relative error of at most 0.0003.
Values sent between devices are 32-bit elements; how exact they have to be, the bound alone decides.
A program may use at most 64 MiB of HBM per device.

v0:
```python
from functools import reduce

import jax
import jax.numpy as jnp
from jax import lax
from jax.sharding import PartitionSpec as P

lattice_moves = [
    (0, 0, 0),
    (1, 0, 0),
    (-1, 0, 0),
    (0, 1, 0),
    (0, -1, 0),
    (0, 0, 1),
    (0, 0, -1),
    (1, 1, 0),
    (-1, -1, 0),
    (1, -1, 0),
    (-1, 1, 0),
    (1, 0, 1),
    (-1, 0, -1),
    (1, 0, -1),
    (-1, 0, 1),
    (0, 1, 1),
    (0, -1, -1),
    (0, 1, -1),
    (0, -1, 1),
]
lattice_weights = [1.0 / 3.0] + [1.0 / 18.0] * 6 + [1.0 / 36.0] * 12
relaxation = 1.6


def with_halo(x, sides, width):
    for axis, dim in sides:
        count, length = (lax.axis_size(axis), x.shape[dim])
        up = [(i, (i + 1) % count) for i in range(count)]
        down = [(j, i) for i, j in up]
        last = lax.slice_in_dim(x, length - width, length, axis=dim)
        leading = lax.slice_in_dim(x, 0, width, axis=dim)
        before = lax.ppermute(last, axis, up)
        after = lax.ppermute(leading, axis, down)
        x = jnp.concatenate([before, x, after], axis=dim)
    return x


def signed_total(pieces, component):
    total = jnp.zeros_like(pieces[0])
    for move, piece in zip(lattice_moves, pieces):
        if move[component] == 1:
            total = total + piece
        elif move[component] == -1:
            total = total - piece
    return total


def lattice_moments(pieces):
    density = reduce(lambda left, right: left + right, pieces)
    velocity_x = signed_total(pieces, 0) / density
    velocity_y = signed_total(pieces, 1) / density
    velocity_z = signed_total(pieces, 2) / density
    return (density, velocity_x, velocity_y, velocity_z)


def collide(pieces):
    density, velocity_x, velocity_y, velocity_z = lattice_moments(pieces)
    speed_sq = velocity_x * velocity_x + velocity_y * velocity_y + velocity_z * velocity_z
    result = []
    for move, weight, piece in zip(lattice_moves, lattice_weights, pieces):
        projected = move[0] * velocity_x + move[1] * velocity_y + move[2] * velocity_z
        balance = (
            weight
            * density
            * (1.0 + 3.0 * projected + 4.5 * projected * projected - 1.5 * speed_sq)
        )
        result.append(piece - relaxation * (piece - balance))
    return result


def stream_axis(pieces, component, padder):
    chosen = [index for index, move in enumerate(lattice_moves) if move[component] != 0]
    padded = padder(jnp.stack([pieces[index] for index in chosen]))
    extent = pieces[0].shape[component]
    result = list(pieces)
    for place, index in enumerate(chosen):
        start = 1 - lattice_moves[index][component]
        result[index] = lax.slice_in_dim(padded[place], start, start + extent, axis=component)
    return result


def on_device(populations):
    pieces = [populations[index] for index in range(19)]
    moments = jnp.stack(lattice_moments(pieces))
    file_order = jnp.transpose(moments, (0, 3, 2, 1))
    moments_slab = lax.all_to_all(file_order, "gx", split_axis=1, concat_axis=3, tiled=True)
    read = stream_axis(pieces, 0, lambda part: with_halo(part, (("gx", 1),), 1))
    read = stream_axis(read, 1, lambda part: with_halo(part, (("gy", 2),), 1))
    read = stream_axis(read, 2, lambda part: with_halo(part, (("gz", 3),), 1))
    populations_next = jnp.stack(collide(read))
    return (populations_next, moments_slab)


def solution(mesh):
    return jax.shard_map(
        on_device,
        mesh=mesh,
        in_specs=(P(None, "gx", "gy", "gz"),),
        out_specs=(P(None, "gx", "gy", "gz"), P(None, ("gz", "gx"), "gy", None)),
        check_vma=False,
    )
```

profile of v0, /device:TPU:0, one launch (start us, length us, event | category | flops | bytes accessed | tf_op | source)
XLA Modules:
  0.0 50.1 jit_solution(12742295588593382738)
XLA Ops:
  0.6 1.0 %slice.286 = f32[8,8,8,128]{3,2,1,0:T(8,128)S(1)} slice(f32[19,8,8,128]{3,2,1,0:T(8,128)} %param.1), slice={[7:15], [0:8], [0:8], [0:128]} | slice | bytes 524288 | tf_op jit(solution)/shard_map/slice | solution.py:91
  1.7 1.5 %constant_dynamic-update-slice_fusion.4 = (f32[10,8,8,128]{3,2,1,0:T(8,128)}, f32[10,8,8,128]{3,2,1,0:T(8,128)S(1)}, f32[2,8,8,128]{3,2,1,0:T(8,128)S(1)}) fusion(f32[19,8,8,128]{3,2,1,0:T(8,128)} %param.1), kind=kLoop, calls=%fused_computation.8 | loop fusion | bytes 393216
  3.2 7.0 %collective-permute-start.1 = (f32[10,1,8,128]{3,2,1,0:T(8,128)S(1)}, f32[10,1,8,128]{3,2,1,0:T(8,128)S(1)}, u32[]{:S(2)}, u32[]{:S(2)}) collective-permute-start(f32[10,1,8,128]{3,2,1,0:T(8,128)S(1)} %get-tuple-element.45), channel_id=1, source_target_pairs={{2,0},{4,2},{6,4},{8,6},{10,8},{12,10},{14,12},{16,14},{18,16},{20... | collective-permute-start | bytes 122888 | tf_op jit(solution)/shard_map/ppermute | solution.py:41
  10.2 1.1 %subtract_divide_fusion.1 = (f32[1,8,8,128]{3,2,1,0:T(8,128)S(1)}, f32[1,8,8,128]{3,2,1,0:T(8,128)S(1)}) fusion(f32[19,8,8,128]{3,2,1,0:T(8,128)} %param.1), kind=kLoop, calls=%fused_computation.241 | loop fusion | flops 229376 | bytes 688128 | tf_op jit(solution)/shard_map/div | solution.py:58
  11.4 0.7 %pad_maximum_fusion.2 = f32[4,8,8,128]{3,2,1,0:T(8,128)} fusion(f32[1,8,8,128]{3,2,1,0:T(8,128)S(1)} %add_divide_fusion, f32[1,8,8,128]{3,2,1,0:T(8,128)S(1)} %subtract_divide_fusion, f32[1,8,8,128]{3,2,1,0:T(8,128)S(1)} %get-tuple-element.4, f32[1,8,8,128]{3,2,1,0:T(8,128)S(1)} %get-tuple-element.5), kind=kLoop, calls=%fused_computation.2 | loop fusion | flops 98304 | bytes 262144 | tf_op jit(solution)/shard_map/stack | solution.py:92
  12.1 2.7 %copy.56 = f32[4,8,8,128]{2,1,0,3:T(8,128)S(1)} copy(f32[4,8,8,128]{3,2,1,0:T(8,128)} %pad_maximum_fusion.2) | data formatting | bytes 262144 | tf_op jit(solution)/shard_map/stack | solution.py:92
  14.8 3.0 %collective-permute-done = f32[10,1,8,128]{3,2,1,0:T(8,128)S(1)} collective-permute-done((f32[10,1,8,128]{3,2,1,0:T(8,128)S(1)}, f32[10,1,8,128]{3,2,1,0:T(8,128)S(1)}, u32[]{:S(2)}, u32[]{:S(2)}) %collective-permute-start) | collective-permute-done | bytes 40992 | tf_op jit(solution)/shard_map/ppermute | solution.py:40
  17.8 0.6 %constant_dynamic-update-slice_fusion.3 = f32[10,8,8,128]{3,2,1,0:T(8,128)} fusion(f32[10,8,8,128]{3,2,1,0:T(8,128)} %get-tuple-element.34, f32[10,1,8,128]{3,2,1,0:T(8,128)S(1)} %collective-permute-done, f32[8,8,8,128]{3,2,1,0:T(8,128)S(1)} %slice.286, f32[2,8,8,128]{3,2,1,0:T(8,128)S(1)} %get-tuple-element.36), kind=kLoop, calls=%fused_computation.7 | loop fusion | flops 16384 | bytes 401408
  18.5 0.6 %constant_dynamic-update-slice_fusion.2 = f32[10,8,8,128]{3,2,1,0:T(8,128)} fusion(f32[10,8,8,128]{3,2,1,0:T(8,128)} %constant_dynamic-update-slice_fusion.3, f32[10,1,8,128]{3,2,1,0:T(8,128)S(1)} %collective-permute-done.1, f32[8,8,8,128]{3,2,1,0:T(8,128)S(1)} %slice.286, f32[2,8,8,128]{3,2,1,0:T(8,128)S(1)} %get-tuple-element.36), kind=kLoop, calls=%fused_computation.6 | loop fusion | flops 16384 | bytes 401408
  19.1 0.6 %constant_dynamic-update-slice_fusion.1 = (f32[10,8,8,128]{3,2,1,0:T(8,128)}, f32[10,8,8,128]{3,2,1,0:T(8,128)S(1)}) fusion(f32[10,8,8,128]{3,2,1,0:T(8,128)} %constant_dynamic-update-slice_fusion.2, f32[10,1,8,128]{3,2,1,0:T(8,128)S(1)} %collective-permute-done, f32[8,8,8,128]{3,2,1,0:T(8,128)S(1)} %slice.286, f32[2,8,8,128]{3,2,1,0:T(8,128)S(1)} %get-tuple-element.36, ...), kind=kLoop, calls=%fused_computation.5 | loop fusion | flops 32768 | bytes 434176
  19.7 0.6 %constant_dynamic-update-slice_fusion = (f32[10,8,8,128]{3,2,1,0:T(8,128)}, f32[10,8,8,128]{3,2,1,0:T(8,128)S(1)}) fusion(f32[10,8,8,128]{3,2,1,0:T(8,128)} %get-tuple-element.39, f32[10,1,8,128]{3,2,1,0:T(8,128)S(1)} %collective-permute-done.1, f32[8,8,8,128]{3,2,1,0:T(8,128)S(1)} %slice.286, f32[2,8,8,128]{3,2,1,0:T(8,128)S(1)} %get-tuple-element.36, ...), kind=kLoop, calls=%fused_computation.4 | loop fusion | flops 32768 | bytes 434176
  20.3 0.7 %slice_dynamic-update-slice_fusion = f32[10,8,8,128]{3,2,1,0:T(8,128)} fusion(f32[10,8,8,128]{3,2,1,0:T(8,128)} %get-tuple-element.37, f32[19,8,8,128]{3,2,1,0:T(8,128)S(1)} %copy-done), kind=kLoop, calls=%fused_computation.3 | loop fusion | bytes 262144 | tf_op jit(solution)/shard_map/stack | solution.py:81
  21.0 1.1 %fusion.152 = (f32[10,8,1,128]{3,2,1,0:T(1,128)S(1)}, f32[10,8,1,128]{3,2,1,0:T(1,128)S(1)}) fusion(f32[10,8,8,128]{3,2,1,0:T(8,128)} %slice_dynamic-update-slice_fusion), kind=kLoop, calls=%fused_computation.254 | loop fusion | bytes 163840 | tf_op jit(solution)/shard_map/slice | solution.py:38
  22.2 1.1 %pad_maximum_fusion = f32[10,8,10,128]{3,2,1,0:T(8,128)S(1)} fusion(f32[10,8,1,128]{3,2,1,0:T(1,128)S(1)} %bitcast.192, f32[10,8,8,128]{3,2,1,0:T(8,128)} %slice_dynamic-update-slice_fusion, f32[10,8,1,128]{3,2,1,0:T(1,128)S(1)} %bitcast.193), kind=kLoop, calls=%fused_computation | loop fusion | flops 204800 | bytes 819200 | tf_op jit(solution)/shard_map/concatenate | solution.py:42
  23.3 0.7 %slice_bitcast_fusion.19 = (f32[8,10,128]{2,1,0:T(8,128)}, f32[8,10,128]{2,1,0:T(8,128)S(1)}, f32[8,10,128]{2,1,0:T(8,128)}, f32[8,10,128]{2,1,0:T(8,128)}, f32[...) fusion(f32[10,8,10,128]{3,2,1,0:T(8,128)S(1)} %pad_maximum_fusion), kind=kLoop, calls=%fused_computation.56 | loop fusion | bytes 819200 | tf_op jit(solution)/shard_map/squeeze | solution.py:86
  24.1 0.9 %fusion.151 = (f32[10,8,8,1]{3,2,1,0:T(8,128)}, f32[10,8,8,1]{3,2,1,0:T(8,128)}) fusion(f32[10,8,8,128]{3,2,1,0:T(8,128)S(1)} %constant_dynamic-update-slice_fusion.5), kind=kLoop, calls=%fused_computation.253 | loop fusion | bytes 10240 | tf_op jit(solution)/shard_map/slice | solution.py:38
  25.0 0.5 %collective-permute-start.5 = (f32[10,8,8,1]{3,2,1,0:T(8,128)}, f32[10,8,8,1]{3,2,1,0:T(8,128)}, u32[]{:S(2)}, u32[]{:S(2)}) collective-permute-start(f32[10,8,8,1]{3,2,1,0:T(8,128)} %get-tuple-element.42), channel_id=1, source_target_pairs={{1,0},{0,1},{3,2},{2,3},{5,4},{4,5},{7,6},{6,7},{9,8},{8,9},{11,10... | collective-permute-start | bytes 7688 | tf_op jit(solution)/shard_map/ppermute | solution.py:41
  25.5 1.5 %bitcast_bitcast_fusion = f32[128,4,8,8]{3,2,1,0:T(8,128)} fusion(f32[4,8,8,128]{2,1,0,3:T(8,128)S(1)} %copy.56), kind=kLoop, calls=%fused_computation.255 | loop fusion | bytes 262144
  27.0 3.3 %reshape.22 = f32[16,1,2048]{2,1,0:T(1,128)} reshape(f32[128,4,8,8]{3,2,1,0:T(8,128)} %bitcast_bitcast_fusion) | data formatting | bytes 262144
  30.4 4.1 %all-to-all-start = ((f32[16,1,2048]{2,1,0:T(1,128)}), f32[16,1,2048]{2,1,0:T(1,128)S(1)}, u32[]{:S(2)}, u32[]{:S(2)}) async-start(f32[16,1,2048]{2,1,0:T(1,128)} %reshape.22), calls=%async_computation | async-start | bytes 262144 | tf_op jit(solution)/shard_map/all_to_all | solution.py:94
  34.6 1.4 %pad_maximum_fusion.1 = f32[10,8,8,130]{3,2,1,0:T(8,128)S(1)} fusion(f32[10,8,8,1]{3,2,1,0:T(8,128)} %collective-permute-done.5, f32[10,8,8,128]{3,2,1,0:T(8,128)S(1)} %constant_dynamic-update-slice_fusion.5, f32[10,8,8,1]{3,2,1,0:T(8,128)} %collective-permute-done.4), kind=kLoop, calls=%fused_computation.1 | loop fusion | flops 166400 | bytes 665600 | tf_op jit(solution)/shard_map/concatenate | solution.py:42
  36.1 0.2 constant_dynamic-update-slice_fusion.32
  36.4 0.1 constant_dynamic-update-slice_fusion.26
  36.6 0.1 constant_dynamic-update-slice_fusion.20
  36.7 0.1 constant_dynamic-update-slice_fusion.19
  36.9 0.1 constant_dynamic-update-slice_fusion.16
  37.1 5.3 %all-to-all-done = f32[16,1,2048]{2,1,0:T(1,128)S(1)} async-done(((f32[16,1,2048]{2,1,0:T(1,128)}), f32[16,1,2048]{2,1,0:T(1,128)S(1)}, u32[]{:S(2)}, u32[]{:S(2)}) %all-to-all-start) | async-done | bytes 131104 | tf_op jit(solution)/shard_map/all_to_all | solution.py:94
  42.3 0.5 %broadcast.211 = f32[]{:T(128)} broadcast(f32[]{:T(128)} %constant.332), dimensions={} | broadcast | bytes 8 | tf_op jit(solution)/shard_map/all_to_all | solution.py:94
  42.9 0.9 %reduce = f32[16,2048]{1,0:T(8,128)S(1)} reduce(f32[16,1,2048]{2,1,0:T(1,128)S(1)} %all-to-all-done, f32[]{:T(128)} %broadcast.211), dimensions={1}, to_apply=%all_to_all.13.reduce_sub_computation | reduce | bytes 262148 | tf_op jit(solution)/shard_map/all_to_all | solution.py:94
  43.8 1.1 %reshape.23 = f32[128,4,8,8]{3,2,1,0:T(8,128)S(1)} reshape(f32[16,2048]{1,0:T(8,128)S(1)} %reduce) | data formatting | bytes 262144
  45.0 1.9 %copy.58 = f32[4,8,8,16,8]{4,3,2,1,0:T(8,128)} copy(f32[4,8,8,16,8]{2,4,0,1,3:T(8,128)S(1)} %bitcast.191) | data formatting | bytes 262144 | tf_op jit(solution)/shard_map/all_to_all | solution.py:94
  46.8 3.2 %all_to_all.16 = f32[4,8,8,128]{3,2,1,0:T(8,128)} reshape(f32[4,8,8,16,8]{4,3,2,1,0:T(8,128)} %copy.58) | data formatting | bytes 262144 | tf_op jit(solution)/shard_map/all_to_all | solution.py:94
  (47 shorter events, 0.6 us)
Async XLA Ops:
  0.6 10.7 %copy-start = (f32[19,8,8,128]{3,2,1,0:T(8,128)S(1)}, f32[19,8,8,128]{3,2,1,0:T(8,128)}, u32[]{:S(2)}) copy-start(f32[19,8,8,128]{3,2,1,0:T(8,128)} %param.1) | copy-start | bytes 1867780
  3.2 15.2 %collective-permute-start.1 = (f32[10,1,8,128]{3,2,1,0:T(8,128)S(1)}, f32[10,1,8,128]{3,2,1,0:T(8,128)S(1)}, u32[]{:S(2)}, u32[]{:S(2)}) collective-permute-start(f32[10,1,8,128]{3,2,1,0:T(8,128)S(1)} %get-tuple-element.45), channel_id=1, source_target_pairs={{2,0},{4,2},{6,4},{8,6},{10,8},{12,10},{14,12},{16,14},{18,16},{20... | collective-permute-start | bytes 122888 | tf_op jit(solution)/shard_map/ppermute | solution.py:41
  10.2 7.6 %collective-permute-start = (f32[10,1,8,128]{3,2,1,0:T(8,128)S(1)}, f32[10,1,8,128]{3,2,1,0:T(8,128)S(1)}, u32[]{:S(2)}, u32[]{:S(2)}) collective-permute-start(f32[10,1,8,128]{3,2,1,0:T(8,128)S(1)} %get-tuple-element.46), channel_id=1, source_target_pairs={{0,2},{2,4},{4,6},{6,8},{8,10},{10,12},{12,14},{14,16},{16,18},{18... | collective-permute-start | bytes 122888 | tf_op jit(solution)/shard_map/ppermute | solution.py:40
  22.1 0.1 collective-permute-start.3
  22.1 0.1 collective-permute-start.2
  25.0 9.5 %collective-permute-start.4 = (f32[10,8,8,1]{3,2,1,0:T(8,128)}, f32[10,8,8,1]{3,2,1,0:T(8,128)}, u32[]{:S(2)}, u32[]{:S(2)}) collective-permute-start(f32[10,8,8,1]{3,2,1,0:T(8,128)} %get-tuple-element.41), channel_id=1, source_target_pairs={{0,1},{1,0},{2,3},{3,2},{4,5},{5,4},{6,7},{7,6},{8,9},{9,8},{10,11... | collective-permute-start | bytes 7688 | tf_op jit(solution)/shard_map/ppermute | solution.py:40
  25.0 9.5 %collective-permute-start.5 = (f32[10,8,8,1]{3,2,1,0:T(8,128)}, f32[10,8,8,1]{3,2,1,0:T(8,128)}, u32[]{:S(2)}, u32[]{:S(2)}) collective-permute-start(f32[10,8,8,1]{3,2,1,0:T(8,128)} %get-tuple-element.42), channel_id=1, source_target_pairs={{1,0},{0,1},{3,2},{2,3},{5,4},{4,5},{7,6},{6,7},{9,8},{8,9},{11,10... | collective-permute-start | bytes 7688 | tf_op jit(solution)/shard_map/ppermute | solution.py:41
  30.4 5.6 %copy-start.1 = (f32[8,10,128]{2,1,0:T(8,128)S(1)}, f32[8,10,128]{2,1,0:T(8,128)}, u32[]{:S(2)}) copy-start(f32[8,10,128]{2,1,0:T(8,128)} %get-tuple-element.26) | copy-start | bytes 122884
  30.4 5.6 %copy-start.2 = (f32[8,10,128]{2,1,0:T(8,128)S(1)}, f32[8,10,128]{2,1,0:T(8,128)}, u32[]{:S(2)}) copy-start(f32[8,10,128]{2,1,0:T(8,128)} %get-tuple-element.27) | copy-start | bytes 122884
  30.4 5.6 %copy-start.3 = (f32[8,10,128]{2,1,0:T(8,128)S(1)}, f32[8,10,128]{2,1,0:T(8,128)}, u32[]{:S(2)}) copy-start(f32[8,10,128]{2,1,0:T(8,128)} %get-tuple-element.28) | copy-start | bytes 122884
  30.4 5.7 %copy-start.4 = (f32[8,10,128]{2,1,0:T(8,128)S(1)}, f32[8,10,128]{2,1,0:T(8,128)}, u32[]{:S(2)}) copy-start(f32[8,10,128]{2,1,0:T(8,128)} %get-tuple-element.33) | copy-start | bytes 122884
  30.4 5.7 %copy-start.5 = (f32[8,10,128]{2,1,0:T(8,128)S(1)}, f32[8,10,128]{2,1,0:T(8,128)}, u32[]{:S(2)}) copy-start(f32[8,10,128]{2,1,0:T(8,128)} %get-tuple-element.24) | copy-start | bytes 122884
  30.4 11.9 %all-to-all-start = ((f32[16,1,2048]{2,1,0:T(1,128)}), f32[16,1,2048]{2,1,0:T(1,128)S(1)}, u32[]{:S(2)}, u32[]{:S(2)}) async-start(f32[16,1,2048]{2,1,0:T(1,128)} %reshape.22), calls=%async_computation | async-start | bytes 262144 | tf_op jit(solution)/shard_map/all_to_all | solution.py:94
  37.1 5.8 %copy-start.6 = (f32[19,8,8,128]{3,2,1,0:T(8,128)}, f32[19,8,8,128]{3,2,1,0:T(8,128)S(1)}, u32[]{:S(2)}) copy-start(f32[19,8,8,128]{3,2,1,0:T(8,128)S(1)} %constant_dynamic-update-slice_fusion.14) | copy-start | bytes 1867780
where the time goes:
time: 50.6 us; the launch traced here: 50.1 us
  local copies, waits for them, and re-layouts  20.5 us (41%)
  starting transfers between devices  11.7 us (23%)
  other arithmetic  8.69 us (17%)
  waiting for transfers between devices  8.31 us (16%)
  between operations  0.93 us (2%)
    unnamed x21, local copies, waits for them, and re-layouts  7.58 us
    ppermute x3, starting transfers between devices, with_halo(): after = lax.ppermute(leading, axis, down)  7.52 us
    all_to_all x3, local copies, waits for them, and re-layouts, on_device(): lax.all_to_all(file_order, 'gx', split_axis=1, concat_axis=3, tiled=True)  5.64 us
    all_to_all x1, waiting for transfers between devices, on_device(): lax.all_to_all(file_order, 'gx', split_axis=1, concat_axis=3, tiled=True)  5.26 us
    all_to_all x1, starting transfers between devices, on_device(): lax.all_to_all(file_order, 'gx', split_axis=1, concat_axis=3, tiled=True)  4.12 us
    unnamed x24, other arithmetic  3.4 us
    ppermute x3, waiting for transfers between devices, with_halo(): before = lax.ppermute(last, axis, up)  3.04 us
    another operation x1, local copies, waits for them, and re-layouts, on_device(): moments = jnp.stack(lattice_moments(pieces))  2.72 us
  transfers between devices with their start and end apart: 7, of which 2 were waited for; matrix products, arithmetic and copies ran while one was open for 25% of the time, Pallas kernels for 0%

commit v1 on v0

v1 whole, which is shorter than its diff:
```python
import functools

import jax
import jax.numpy as jnp
from jax import lax
from jax.experimental import pallas as pl
from jax.experimental.pallas import tpu as pltpu
from jax.sharding import PartitionSpec as P

MESH = pl.DeviceIdType.MESH

lattice_moves = [
    (0, 0, 0),
    (1, 0, 0),
    (-1, 0, 0),
    (0, 1, 0),
    (0, -1, 0),
    (0, 0, 1),
    (0, 0, -1),
    (1, 1, 0),
    (-1, -1, 0),
    (1, -1, 0),
    (-1, 1, 0),
    (1, 0, 1),
    (-1, 0, -1),
    (1, 0, -1),
    (-1, 0, 1),
    (0, 1, 1),
    (0, -1, -1),
    (0, 1, -1),
    (0, -1, 1),
]
lattice_weights = [1.0 / 3.0] + [1.0 / 18.0] * 6 + [1.0 / 36.0] * 12
relaxation = 1.6
count_q = len(lattice_moves)


def movers(component, sign):
    return [q for q, move in enumerate(lattice_moves) if move[component] == sign]


def place_in(q, component):
    return movers(component, lattice_moves[q][component]).index(q)


def side(sign):
    return 0 if sign > 0 else 1


edges_xz = [q for q, m in enumerate(lattice_moves) if m[0] and m[2]]
edges_xy = [q for q, m in enumerate(lattice_moves) if m[0] and m[1]]
edges_yz = [q for q, m in enumerate(lattice_moves) if m[1] and m[2]]


def total(terms):
    terms = list(terms)
    while len(terms) > 1:
        terms = [
            terms[i] + terms[i + 1] if i + 1 < len(terms) else terms[i]
            for i in range(0, len(terms), 2)
        ]
    return terms[0]


def moments_of(f):
    density = total(f)
    inverse = 1.0 / density
    velocity = []
    for component in range(3):
        plus = total(f[q] for q in movers(component, 1))
        minus = total(f[q] for q in movers(component, -1))
        velocity.append((plus - minus) * inverse)
    return density, velocity


def collided(f):
    density, velocity = moments_of(f)
    speed_sq = velocity[0] * velocity[0] + velocity[1] * velocity[1] + velocity[2] * velocity[2]
    base = 1.0 - 1.5 * speed_sq
    scaled = {w: (relaxation * w) * density for w in set(lattice_weights)}
    keep = 1.0 - relaxation
    result = [None] * count_q
    result[0] = keep * f[0] + scaled[lattice_weights[0]] * base
    for q in range(1, count_q, 2):
        move = lattice_moves[q]
        projected = None
        for component in range(3):
            if move[component] == 0:
                continue
            if projected is None:
                projected = velocity[component] if move[component] > 0 else -velocity[component]
            elif move[component] > 0:
                projected = projected + velocity[component]
            else:
                projected = projected - velocity[component]
        even = base + 4.5 * (projected * projected)
        odd = 3.0 * projected
        weight = scaled[lattice_weights[q]]
        result[q] = keep * f[q] + weight * (even + odd)
        result[q + 1] = keep * f[q + 1] + weight * (even - odd)
    return result


def rolled(v, shift, axis):
    return pltpu.roll(v, shift % v.shape[axis], axis)


def kernel(axes, sizes, pop_hbm, next_ref, slab_ref,
           pop, out_vm, slab_vm, face_x, edge_xz, pack_z, face_z, send_m, recv_m, mid,
           row_y, face_y, edge_xy, edge_yz,
           load_sem, store_sem, send_sem, recv_sem, send_m_sem, recv_m_sem):
    nx, ny, nz = (sizes[a] for a in axes)
    here = tuple(lax.axis_index(a) for a in axes)
    _, lx, ly, lz = pop.shape
    split_y = ny > 1

    def device_at(offset):
        return tuple(
            lax.rem(h + (o % n), n) if o % n else h
            for h, o, n in zip(here, offset, (nx, ny, nz))
        )

    offsets = [(k, 0, 0) for k in range(1, nx)]
    offsets += [(0, 0, 1), (0, 0, -1)]
    offsets += [lattice_moves[q] for q in edges_xz]
    if split_y:
        offsets += [(0, 1, 0), (0, -1, 0)]
        offsets += [lattice_moves[q] for q in edges_xy + edges_yz]
    partners = sorted({(a % nx, b % ny, c % nz) for a, b, c in offsets})
    barrier = pltpu.get_barrier_semaphore()
    for offset in partners:
        pl.semaphore_signal(barrier, inc=1, device_id=device_at(offset), device_id_type=MESH)

    load = pltpu.make_async_copy(pop_hbm, pop, load_sem)
    load.start()
    load.wait()

    lane = lax.broadcasted_iota(jnp.int32, (ly, lz), 1)
    row = lax.broadcasted_iota(jnp.int32, (ly, lz), 0)

    for sign in (1, -1):
        at = lz - 1 if sign > 0 else 0
        packed = jnp.zeros((ly, lz), jnp.float32)
        for i, q in enumerate(movers(2, sign)):
            for x in range(lx):
                k = i * lx + x
                packed = jnp.where(lane == k, rolled(pop[q, x], k - at, 1), packed)
        pack_z[side(sign)] = packed
    if split_y:
        for sign in (1, -1):
            at = ly - 1 if sign > 0 else 0
            for i, q in enumerate(movers(1, sign)):
                for x in range(lx):
                    row_y[side(sign), i, x:x + 1, :] = pop[q, x, at:at + 1, :]

    values = [[None] * lx for _ in range(4)]
    for x in range(lx):
        density, velocity = moments_of([pop[q, x] for q in range(count_q)])
        for c, v in enumerate([density] + velocity):
            values[c][x] = v
    for c in range(4):
        tiles = values[c]
        step = 1
        while step < lx:
            upper = (lane & step) != 0
            fresh = list(tiles)
            for x in range(lx):
                if x & step:
                    continue
                a, b = tiles[x], tiles[x + step]
                fresh[x] = jnp.where(upper, rolled(b, step, 1), a)
                fresh[x + step] = jnp.where(upper, b, rolled(a, -step, 1))
            tiles = fresh
            step *= 2
        for z in range(lx):
            mid[c, z * ly:(z + 1) * ly, :] = tiles[z]
    for p in range(2):
        square = mid[2 * p:2 * p + 2].reshape(lz, lz).T
        for j in range(nx):
            send_m[j, p] = square[j * lx:(j + 1) * lx]

    pl.semaphore_wait(barrier, len(partners))

    me = here[0]
    outgoing = []
    count = [0]

    def send(src, dst, offset):
        s = count[0]
        count[0] += 1
        copy = pltpu.make_async_remote_copy(
            src_ref=src, dst_ref=dst, send_sem=send_sem.at[s], recv_sem=recv_sem.at[s],
            device_id=device_at(offset), device_id_type=MESH)
        copy.start()
        outgoing.append(copy)
        return copy

    moment_copies = []

    def send_moments(k):
        target = device_at((k, 0, 0))
        copy = pltpu.make_async_remote_copy(
            src_ref=send_m.at[target[0]], dst_ref=recv_m.at[me],
            send_sem=send_m_sem.at[k], recv_sem=recv_m_sem.at[k],
            device_id=target, device_id_type=MESH)
        copy.start()
        moment_copies.append(copy)

    z_copies, x_copies = [], []
    for sign in (1, -1):
        s = side(sign)
        z_copies.append(send(pack_z.at[s], face_z.at[s], (0, 0, sign)))
    for sign in (1, -1):
        s, at = side(sign), lx - 1 if sign > 0 else 0
        for i, q in enumerate(movers(0, sign)):
            x_copies.append(send(pop.at[q, at], face_x.at[s, i], (sign, 0, 0)))
    for i, q in enumerate(edges_xz):
        at = lx - 1 if lattice_moves[q][0] > 0 else 0
        x_copies.append(send(pop.at[q, at], edge_xz.at[i], lattice_moves[q]))
    if split_y:
        for sign in (1, -1):
            s = side(sign)
            z_copies.append(send(row_y.at[s], face_y.at[s], (0, sign, 0)))
        for i, q in enumerate(edges_yz):
            s = side(lattice_moves[q][2])
            z_copies.append(send(pack_z.at[s], edge_yz.at[i], lattice_moves[q]))
        for i, q in enumerate(edges_xy):
            s = side(lattice_moves[q][1])
            x_copies.append(send(row_y.at[s, place_in(q, 1)], edge_xy.at[i], lattice_moves[q]))
    for k in sorted(range(1, nx), key=lambda k: abs(k - nx // 2)):
        send_moments(k)
    recv_m[me] = send_m[me]

    def streamed(q, x):
        cx, cy, cz = lattice_moves[q]
        sx = x - cx
        inside = 0 <= sx < lx
        sx_wrapped = sx % lx
        v = pop[q, sx] if inside else face_x[side(cx), place_in(q, 0)]
        if cy and split_y:
            at = ly - 1 if cy > 0 else 0
            if inside:
                other = face_y[side(cy), place_in(q, 1), sx:sx + 1, :]
            else:
                other = edge_xy[edges_xy.index(q), sx_wrapped:sx_wrapped + 1, :]
            v = jnp.where(row == at, jnp.broadcast_to(other, v.shape), v)
        if cz:
            at = lz - 1 if cz > 0 else 0
            if inside:
                other = face_z[side(cz)]
                if cy and split_y:
                    at_y = ly - 1 if cy > 0 else 0
                    other = jnp.where(row == at_y, edge_yz[edges_yz.index(q)], other)
                k = place_in(q, 2) * lx + sx
                other = rolled(other, at - k, 1)
            else:
                other = edge_xz[edges_xz.index(q)]
            v = jnp.where(lane == at, other, v)
        if cy:
            v = rolled(v, cy, 0)
        if cz:
            v = rolled(v, cz, 1)
        return v

    def advance(x):
        result = collided([streamed(q, x) for q in range(count_q)])
        for q in range(count_q):
            out_vm[q, x] = result[q]

    for copy in z_copies:
        copy.wait_recv()
    for x in range(1, lx - 1):
        advance(x)
    for copy in x_copies:
        copy.wait_recv()
    advance(0)
    advance(lx - 1)
    store_next = pltpu.make_async_copy(out_vm, next_ref, store_sem.at[0])
    store_next.start()

    for copy in moment_copies:
        copy.wait_recv()
    for p in range(2):
        square = recv_m[:, p].reshape(lz, lz).T
        slab_vm[2 * p:2 * p + 2] = square.reshape(2, lx, ly, lz)
    store_slab = pltpu.make_async_copy(slab_vm, slab_ref, store_sem.at[1])
    store_slab.start()
    for copy in outgoing + moment_copies:
        copy.wait_send()
    store_next.wait()
    store_slab.wait()


def on_device(axes, sizes, populations):
    q, lx, ly, lz = populations.shape
    nx = sizes[axes[0]]
    messages = 2 + 10 + 4
    if sizes[axes[1]] > 1:
        messages += 2 + 4 + 4
    f32 = jnp.float32
    tile = (ly, lz)
    return pl.pallas_call(
        functools.partial(kernel, axes, sizes),
        out_shape=(
            jax.ShapeDtypeStruct(populations.shape, f32),
            jax.ShapeDtypeStruct((4, lz // nx, ly, lx * nx), f32),
        ),
        in_specs=[pl.BlockSpec(memory_space=pl.ANY)],
        out_specs=(pl.BlockSpec(memory_space=pl.ANY),) * 2,
        scratch_shapes=[
            pltpu.VMEM(populations.shape, f32),
            pltpu.VMEM(populations.shape, f32),
            pltpu.VMEM((4, lz // nx, ly, lx * nx), f32),
            pltpu.VMEM((2, 5) + tile, f32),
            pltpu.VMEM((4,) + tile, f32),
            pltpu.VMEM((2,) + tile, f32),
            pltpu.VMEM((2,) + tile, f32),
            pltpu.VMEM((nx, 2, lx, lz), f32),
            pltpu.VMEM((nx, 2, lx, lz), f32),
            pltpu.VMEM((4, lx * ly, lz), f32),
            pltpu.VMEM((2, 5, lx, lz), f32),
            pltpu.VMEM((2, 5, lx, lz), f32),
            pltpu.VMEM((4, lx, lz), f32),
            pltpu.VMEM((4,) + tile, f32),
            pltpu.SemaphoreType.DMA,
            pltpu.SemaphoreType.DMA((2,)),
            pltpu.SemaphoreType.DMA((messages,)),
            pltpu.SemaphoreType.DMA((messages,)),
            pltpu.SemaphoreType.DMA((nx,)),
            pltpu.SemaphoreType.DMA((nx,)),
        ],
        compiler_params=pltpu.CompilerParams(collective_id=0, has_side_effects=True),
        name="lattice_step",
    )(populations)


def solution(mesh):
    axes = tuple(mesh.axis_names)
    sizes = dict(mesh.shape)
    return jax.shard_map(
        functools.partial(on_device, axes, sizes),
        mesh=mesh,
        in_specs=(P(None, "gx", "gy", "gz"),),
        out_specs=(P(None, "gx", "gy", "gz"), P(None, ("gz", "gx"), "gy", None)),
        check_vma=False,
    )
```

time: 50.6 us -> 16.8 us (0.33)
  local copies, waits for them, and re-layouts: 20.5 us -> 2.65 us
  Pallas kernels: 0 us -> 13.3 us
  starting transfers between devices: 11.7 us -> 0 us
  other arithmetic: 8.69 us -> 0 us
  waiting for transfers between devices: 8.31 us -> 0 us
    pallas_call x0 -> x1, Pallas kernels: none -> 13.3 us  [on_device(): pl.pallas_call(functools.partial(kernel, axes, sizes), out_shape=(jax.Sha...]
    ppermute x6 -> x0, starting transfers between devices: 7.53 us -> none  [the longest x3 7.52 us: with_halo(): after = lax.ppermute(leading, axis, down)]
    all_to_all x3 -> x0, local copies, waits for them, and re-layouts: 5.64 us -> none  [on_device(): lax.all_to_all(file_order, 'gx', split_axis=1, concat_axis=3, tiled=True)]
    all_to_all x1 -> x0, waiting for transfers between devices: 5.26 us -> none  [on_device(): lax.all_to_all(file_order, 'gx', split_axis=1, concat_axis=3, tiled=True)]
    unnamed x21 -> x4, local copies, waits for them, and re-layouts: 7.58 us -> 2.65 us
    all_to_all x1 -> x0, starting transfers between devices: 4.12 us -> none  [on_device(): lax.all_to_all(file_order, 'gx', split_axis=1, concat_axis=3, tiled=True)]
    unnamed x24 -> x0, other arithmetic: 3.4 us -> none
    another operation x3 -> x0, local copies, waits for them, and re-layouts: 3.39 us -> none  [the longest x1 2.72 us: on_device(): moments = jnp.stack(lattice_moments(pieces))]
  transfers between devices with their start and end apart: 7 -> 0, of which waited for: 2 -> 0; matrix products, arithmetic and copies ran while one was open for 25% -> 0% of each run, Pallas kernels for 0% -> 0%
where the time goes in v1:
time: 16.8 us; the launch traced here: 16.6 us
  Pallas kernels  13.3 us (79%)
  local copies, waits for them, and re-layouts  2.65 us (16%)
  between operations  0.65 us (4%)
    pallas_call x1, Pallas kernels, on_device(): pl.pallas_call(functools.partial(kernel, axes, sizes), out_shape=(jax.Sha...  13.3 us
    unnamed x4, local copies, waits for them, and re-layouts  2.65 us

profile of v1, /device:TPU:0, one launch (start us, length us, event | category | flops | bytes accessed | tf_op | source)
XLA Modules:
  0.0 16.6 jit_solution(16123603669014829191)
XLA Ops:
  0.6 13.3 %lattice_step.1 = (f32[19,8,8,128]{3,2,1,0:T(8,128)}, f32[4,8,8,128]{3,2,1,0:T(8,128)}) custom-call(f32[19,8,8,128]{3,2,1,0:T(8,128)} %pop_hbm.1), custom_call_target="tpu_custom_call" | custom-call | tf_op jit(solution)/shard_map/lattice_step/pallas_call | solution.py:302
  13.9 0.0 copy-start
  13.9 2.0 %copy.5 = f32[19,8,8,128]{3,2,1,0:T(8,128)} copy(f32[19,8,8,128]{3,2,1,0:T(8,128)} %get-tuple-element.4) | data formatting | bytes 1245184
  15.9 0.0 copy-done
  15.9 0.7 %copy.6 = f32[4,8,8,128]{3,2,1,0:T(8,128)} copy(f32[4,8,8,128]{3,2,1,0:T(8,128)S(1)} %copy-done) | data formatting | bytes 262144
Async XLA Ops:
  13.9 2.0 %copy-start = (f32[4,8,8,128]{3,2,1,0:T(8,128)S(1)}, f32[4,8,8,128]{3,2,1,0:T(8,128)}, u32[]{:S(2)}) copy-start(f32[4,8,8,128]{3,2,1,0:T(8,128)} %get-tuple-element.5) | copy-start | bytes 393220

commit v2 on v1

--- a/solution.py
+++ b/solution.py
@@ -105,10 +105,10 @@
     return pltpu.roll(v, shift % v.shape[axis], axis)
 
 
-def kernel(axes, sizes, pop_hbm, next_ref, slab_ref,
-           pop, out_vm, slab_vm, face_x, edge_xz, pack_z, face_z, send_m, recv_m, mid,
+def kernel(axes, sizes, pop_hbm, out_vm, slab_vm,
+           pop, face_x, edge_xz, pack_z, face_z, send_m, recv_m, mid,
            row_y, face_y, edge_xy, edge_yz,
-           load_sem, store_sem, send_sem, recv_sem, send_m_sem, recv_m_sem):
+           load_sem, send_sem, recv_sem, send_m_sem, recv_m_sem):
     nx, ny, nz = (sizes[a] for a in axes)
     here = tuple(lax.axis_index(a) for a in axes)
     _, lx, ly, lz = pop.shape
@@ -275,20 +275,25 @@
         copy.wait_recv()
     advance(0)
     advance(lx - 1)
-    store_next = pltpu.make_async_copy(out_vm, next_ref, store_sem.at[0])
-    store_next.start()
 
     for copy in moment_copies:
         copy.wait_recv()
     for p in range(2):
         square = recv_m[:, p].reshape(lz, lz).T
         slab_vm[2 * p:2 * p + 2] = square.reshape(2, lx, ly, lz)
-    store_slab = pltpu.make_async_copy(slab_vm, slab_ref, store_sem.at[1])
-    store_slab.start()
     for copy in outgoing + moment_copies:
         copy.wait_send()
-    store_next.wait()
-    store_slab.wait()
+
+
+def write_out(next_vm, slab_vm, next_ref, slab_ref, sems):
+    stores = [
+        pltpu.make_async_copy(next_vm, next_ref, sems.at[0]),
+        pltpu.make_async_copy(slab_vm, slab_ref, sems.at[1]),
+    ]
+    for store in stores:
+        store.start()
+    for store in stores:
+        store.wait()
 
 
 def on_device(axes, sizes, populations):
@@ -299,18 +304,16 @@
         messages += 2 + 4 + 4
     f32 = jnp.float32
     tile = (ly, lz)
-    return pl.pallas_call(
+    held = pl.pallas_call(
         functools.partial(kernel, axes, sizes),
         out_shape=(
-            jax.ShapeDtypeStruct(populations.shape, f32),
-            jax.ShapeDtypeStruct((4, lz // nx, ly, lx * nx), f32),
+            pltpu.VMEM(populations.shape, f32),
+            pltpu.VMEM((4, lz // nx, ly, lx * nx), f32),
         ),
         in_specs=[pl.BlockSpec(memory_space=pl.ANY)],
-        out_specs=(pl.BlockSpec(memory_space=pl.ANY),) * 2,
+        out_specs=(pl.BlockSpec(memory_space=pltpu.VMEM),) * 2,
         scratch_shapes=[
             pltpu.VMEM(populations.shape, f32),
-            pltpu.VMEM(populations.shape, f32),
-            pltpu.VMEM((4, lz // nx, ly, lx * nx), f32),
             pltpu.VMEM((2, 5) + tile, f32),
             pltpu.VMEM((4,) + tile, f32),
             pltpu.VMEM((2,) + tile, f32),
@@ -323,7 +326,6 @@
             pltpu.VMEM((4, lx, lz), f32),
             pltpu.VMEM((4,) + tile, f32),
             pltpu.SemaphoreType.DMA,
-            pltpu.SemaphoreType.DMA((2,)),
             pltpu.SemaphoreType.DMA((messages,)),
             pltpu.SemaphoreType.DMA((messages,)),
             pltpu.SemaphoreType.DMA((nx,)),
@@ -332,6 +334,15 @@
         compiler_params=pltpu.CompilerParams(collective_id=0, has_side_effects=True),
         name="lattice_step",
     )(populations)
+    held = [pltpu.with_memory_space_constraint(h, pltpu.VMEM) for h in held]
+    return pl.pallas_call(
+        write_out,
+        out_shape=tuple(jax.ShapeDtypeStruct(h.shape, f32) for h in held),
+        in_specs=[pl.BlockSpec(memory_space=pltpu.VMEM)] * 2,
+        out_specs=(pl.BlockSpec(memory_space=pl.ANY),) * 2,
+        scratch_shapes=[pltpu.SemaphoreType.DMA((2,))],
+        name="write_out",
+    )(*held)
 
 
 def solution(mesh):

time: 16.8 us -> 14.4 us (0.86)
  local copies, waits for them, and re-layouts: 2.65 us -> 0 us
  Pallas kernels: 13.3 us -> 13.6 us
    unnamed x4 -> x0, local copies, waits for them, and re-layouts: 2.65 us -> none
    pallas_call x1 -> x2, Pallas kernels: 13.3 us -> 13.6 us  [the longest x1 12.7 us: on_device(): pl.pallas_call(functools.partial(kernel, axes, sizes), out_shape=(pltpu.V...]
where the time goes in v2:
time: 14.4 us; the launch traced here: 14.2 us
  Pallas kernels  13.6 us (94%)
  between operations  0.64 us (4%)
    pallas_call x1, Pallas kernels, on_device(): pl.pallas_call(functools.partial(kernel, axes, sizes), out_shape=(pltpu.V...  12.7 us
    pallas_call x1, Pallas kernels, on_device(): pl.pallas_call(write_out, out_shape=tuple((jax.ShapeDtypeStruct(h.shape,...  0.88 us

profile of v2, /device:TPU:0, one launch (start us, length us, event | category | flops | bytes accessed | tf_op | source)
XLA Modules:
  0.0 14.2 jit_solution(6327664456583664950)
XLA Ops:
  0.6 12.7 %lattice_step.1 = (f32[19,8,8,128]{3,2,1,0:T(8,128)S(1)}, f32[4,8,8,128]{3,2,1,0:T(8,128)S(1)}) custom-call(f32[19,8,8,128]{3,2,1,0:T(8,128)} %pop_hbm.1), custom_call_target="tpu_custom_call" | custom-call | tf_op jit(solution)/shard_map/lattice_step/pallas_call | solution.py:307
  13.3 0.9 %write_out.1 = (f32[19,8,8,128]{3,2,1,0:T(8,128)}, f32[4,8,8,128]{3,2,1,0:T(8,128)}) custom-call(f32[19,8,8,128]{3,2,1,0:T(8,128)S(1)} %get-tuple-element.4.next_vm, f32[4,8,8,128]{3,2,1,0:T(8,128)S(1)} %get-tuple-element.5.slab_vm), custom_call_target="tpu_custom_call" | custom-call | tf_op jit(solution)/shard_map/write_out/pallas_call | solution.py:338

commit v3 on v2

--- a/solution.py
+++ b/solution.py
@@ -105,8 +105,19 @@
     return pltpu.roll(v, shift % v.shape[axis], axis)
 
 
+def paired(at, k, n):
+    if n & (n - 1):
+        return lax.rem(at + k, n)
+    bit = 1
+    while bit < n:
+        if k & bit:
+            at = at + bit - 2 * bit * lax.rem(at // bit, 2)
+        bit *= 2
+    return at
+
+
 def kernel(axes, sizes, pop_hbm, out_vm, slab_vm,
-           pop, face_x, edge_xz, pack_z, face_z, send_m, recv_m, mid,
+           pop, face_x, edge_xz, pack_x, pack_z, face_z, send_m, recv_m, mid,
            row_y, face_y, edge_xy, edge_yz,
            load_sem, send_sem, recv_sem, send_m_sem, recv_m_sem):
     nx, ny, nz = (sizes[a] for a in axes)
@@ -146,6 +157,10 @@
                 k = i * lx + x
                 packed = jnp.where(lane == k, rolled(pop[q, x], k - at, 1), packed)
         pack_z[side(sign)] = packed
+    for sign in (1, -1):
+        at = lx - 1 if sign > 0 else 0
+        up, down = (lattice_moves.index((sign, 0, cz)) for cz in (1, -1))
+        pack_x[side(sign)] = jnp.where(lane == lz - 1, pop[up, at], pop[down, at])
     if split_y:
         for sign in (1, -1):
             at = ly - 1 if sign > 0 else 0
@@ -198,7 +213,7 @@
     moment_copies = []
 
     def send_moments(k):
-        target = device_at((k, 0, 0))
+        target = (paired(here[0], k, nx),) + here[1:]
         copy = pltpu.make_async_remote_copy(
             src_ref=send_m.at[target[0]], dst_ref=recv_m.at[me],
             send_sem=send_m_sem.at[k], recv_sem=recv_m_sem.at[k],
@@ -214,9 +229,12 @@
         s, at = side(sign), lx - 1 if sign > 0 else 0
         for i, q in enumerate(movers(0, sign)):
             x_copies.append(send(pop.at[q, at], face_x.at[s, i], (sign, 0, 0)))
+    edge_slot = {}
     for i, q in enumerate(edges_xz):
-        at = lx - 1 if lattice_moves[q][0] > 0 else 0
-        x_copies.append(send(pop.at[q, at], edge_xz.at[i], lattice_moves[q]))
+        cx, _, cz = lattice_moves[q]
+        if (cx, cz % nz) not in edge_slot:
+            edge_slot[cx, cz % nz] = i
+            x_copies.append(send(pack_x.at[side(cx)], edge_xz.at[i], lattice_moves[q]))
     if split_y:
         for sign in (1, -1):
             s = side(sign)
@@ -227,7 +245,12 @@
         for i, q in enumerate(edges_xy):
             s = side(lattice_moves[q][1])
             x_copies.append(send(row_y.at[s, place_in(q, 1)], edge_xy.at[i], lattice_moves[q]))
-    for k in sorted(range(1, nx), key=lambda k: abs(k - nx // 2)):
+    order = sorted(range(1, nx), key=lambda k: (k % 2 == 0, -bin(k).count("1"), abs(k - 11)))
+    early = [k for k in order if bin(k).count("1") > 2]
+    order = early + [k for k in order if k not in early]
+    for k in early:
+        send_moments(k)
+    for k in order[len(early):]:
         send_moments(k)
     recv_m[me] = send_m[me]
 
@@ -254,7 +277,7 @@
                 k = place_in(q, 2) * lx + sx
                 other = rolled(other, at - k, 1)
             else:
-                other = edge_xz[edges_xz.index(q)]
+                other = edge_xz[edge_slot[cx, cz % nz]]
             v = jnp.where(lane == at, other, v)
         if cy:
             v = rolled(v, cy, 0)
@@ -316,6 +339,7 @@
             pltpu.VMEM(populations.shape, f32),
             pltpu.VMEM((2, 5) + tile, f32),
             pltpu.VMEM((4,) + tile, f32),
+            pltpu.VMEM((2,) + tile, f32),
             pltpu.VMEM((2,) + tile, f32),
             pltpu.VMEM((2,) + tile, f32),
             pltpu.VMEM((nx, 2, lx, lz), f32),

time: 14.4 us -> 13.8 us (0.958)
  Pallas kernels: 13.6 us -> 13 us
    pallas_call x1, Pallas kernels: 12.7 us -> 12.1 us  [on_device(): pl.pallas_call(functools.partial(kernel, axes, sizes), out_shape=(pltpu.V...]
where the time goes in v3:
time: 13.8 us; the launch traced here: 13.6 us
  Pallas kernels  13 us (94%)
  between operations  0.64 us (5%)
    pallas_call x1, Pallas kernels, on_device(): pl.pallas_call(functools.partial(kernel, axes, sizes), out_shape=(pltpu.V...  12.1 us
    pallas_call x1, Pallas kernels, on_device(): pl.pallas_call(write_out, out_shape=tuple((jax.ShapeDtypeStruct(h.shape,...  0.88 us

profile of v3, /device:TPU:0, one launch (start us, length us, event | category | flops | bytes accessed | tf_op | source)
XLA Modules:
  0.0 13.6 jit_solution(835407719020096488)
XLA Ops:
  0.6 12.1 %lattice_step.1 = (f32[19,8,8,128]{3,2,1,0:T(8,128)S(1)}, f32[4,8,8,128]{3,2,1,0:T(8,128)S(1)}) custom-call(f32[19,8,8,128]{3,2,1,0:T(8,128)} %pop_hbm.1), custom_call_target="tpu_custom_call" | custom-call | tf_op jit(solution)/shard_map/lattice_step/pallas_call | solution.py:330
  12.7 0.9 %write_out.1 = (f32[19,8,8,128]{3,2,1,0:T(8,128)}, f32[4,8,8,128]{3,2,1,0:T(8,128)}) custom-call(f32[19,8,8,128]{3,2,1,0:T(8,128)S(1)} %get-tuple-element.4.next_vm, f32[4,8,8,128]{3,2,1,0:T(8,128)S(1)} %get-tuple-element.5.slab_vm), custom_call_target="tpu_custom_call" | custom-call | tf_op jit(solution)/shard_map/write_out/pallas_call | solution.py:362
